TPU v7x, 32 devices: a whole 2x2x4 slice. The times are simulated.
32 devices in a mesh: dp: 8 (over y, x, core), mp: 4 (over z).
Axes of the slice: x: 2, y: 2, z: 4, core: 2. Of those that a mesh axis runs over, the one named last changes fastest.
Arguments:
- tokens: bfloat16 [4096, 1024], P('dp', 'mp'), may hold values from -150 to 150
- pre_gain: bfloat16 [1024], P('mp'), may hold values from 0.25 to 1.75
- input_weight: bfloat16 [3, 1024, 1024], P(None, 'dp', 'mp'), may hold values from -0.125 to 0.125
- output_weight: bfloat16 [1024, 1024], P('mp', 'dp'), may hold values from -1 to 1
- position_bias: bfloat16 [16, 512, 512], P('mp'), may hold values from -3 to 353
- post_gain: bfloat16 [1024], P('mp'), may hold values from 0.25 to 1.75
Outputs:
- stream: bfloat16 [4096, 1024], P('dp', 'mp')
- normed: bfloat16 [4096, 1024], P('dp', 'mp')
All inputs are finite; a program needn't handle non-finite values.
Results may differ from a plain program's by a relative error of at most 0.013.
Values may be sent and summed in bfloat16 or wider, within the bound.
A program may use at most 64 MiB of HBM per device.

v0:
```python
import jax
import jax.numpy as jnp
from jax import lax
from jax.sharding import PartitionSpec as P

epsilon = 1e-06


def attend_all(mixed_heads, position_bias):
    row_count = mixed_heads.shape[1]
    inner_width = mixed_heads.shape[2]
    head_count = position_bias.shape[0]
    seq_len = position_bias.shape[1]
    grouped = mixed_heads.reshape(
        3, row_count // seq_len, seq_len, head_count, inner_width // head_count
    )
    bias_wide = position_bias.astype(jnp.float32)

    def one_sequence(sequence):
        sequence_block = lax.dynamic_index_in_dim(grouped, sequence, 1, keepdims=False)
        scores = (
            jnp.einsum(
                "qhd,khd->hqk",
                sequence_block[0],
                sequence_block[1],
                preferred_element_type=jnp.float32,
            )
            + bias_wide
        )
        row_max = jnp.max(scores, axis=2, keepdims=True)
        weights = jnp.exp(scores - row_max)
        probabilities = (weights / jnp.sum(weights, axis=2, keepdims=True)).astype(jnp.bfloat16)
        context = jnp.einsum(
            "hqk,khd->qhd", probabilities, sequence_block[2], preferred_element_type=jnp.float32
        )
        return context.reshape(seq_len, inner_width).astype(jnp.bfloat16)

    stacked = lax.map(one_sequence, jnp.arange(row_count // seq_len, dtype=jnp.int32))
    return stacked.reshape(row_count, inner_width)


def on_device(tokens, pre_gain, input_weight, output_weight, position_bias, post_gain):
    rows_all, gain_all = (
        lax.all_gather(tokens, "mp", axis=1, tiled=True),
        lax.all_gather(pre_gain, "mp", axis=0, tiled=True),
    )
    widened = rows_all.astype(jnp.float32)
    inverse_rms = lax.rsqrt(jnp.mean(widened * widened, axis=1, keepdims=True) + epsilon)
    normed_in = (widened * inverse_rms * gain_all.astype(jnp.float32)).astype(jnp.bfloat16)
    feature_count = tokens.shape[1]
    projected = jnp.einsum(
        "td,kdi->kti",
        normed_in,
        lax.all_gather(input_weight, "dp", axis=1, tiled=True),
        preferred_element_type=jnp.float32,
    )
    context = attend_all(projected.astype(jnp.bfloat16), position_bias)
    partial_value = jnp.dot(
        context,
        lax.all_gather(output_weight, "dp", axis=1, tiled=True),
        preferred_element_type=jnp.float32,
    )
    attention_out = lax.psum_scatter(
        partial_value.astype(jnp.bfloat16), "mp", scatter_dimension=1, tiled=True
    ).astype(jnp.float32)
    stream = (tokens.astype(jnp.float32) + attention_out).astype(jnp.bfloat16)
    restored = lax.optimization_barrier(stream).astype(jnp.float32)
    squares = lax.psum(jnp.sum(restored * restored, axis=1), "mp")
    post_rms = lax.rsqrt(squares[:, None] / (feature_count * lax.axis_size("mp")) + epsilon)
    normed = (restored * post_rms * post_gain.astype(jnp.float32)).astype(jnp.bfloat16)
    return (stream, normed)


def solution(mesh):
    return jax.shard_map(
        on_device,
        mesh=mesh,
        in_specs=(
            P("dp", "mp"),
            P("mp"),
            P(None, "dp", "mp"),
            P("mp", "dp"),
            P("mp", None, None),
            P("mp"),
        ),
        out_specs=(P("dp", "mp"), P("dp", "mp")),
        check_vma=False,
    )
```

profile of v0, /device:TPU:0, one launch (start us, length us, event | category | flops | bytes accessed | tf_op | source)
XLA Modules:
  0.0 123.4 jit_solution(2190378064825369234)
XLA Ops:
  7.2 0.0 all-gather.4.cloned.1.call-start
  7.2 0.7 all-gather.4.cloned.1.call-update
  7.9 0.0 all-gather.6.cloned.1.call-start
  7.9 1.7 %copy.11 = bf16[3,128,256]{1,2,0:T(8,128)(2,1)} copy(bf16[3,128,256]{2,1,0:T(8,128)(2,1)} %param.8) | data formatting | bytes 393216 | tf_op args[2]
  9.7 0.0 all-gather.6.cloned.1.call-update
  9.7 0.0 reduce-scatter.2.cloned.1.call-start
  9.8 0.7 reshape.34
  10.4 12.6 %all-gather = bf16[4,1,256]{2,1,0:T(2,128)(2,1)S(1)} all-gather(bf16[1,1,256]{2,1,0:T(2,128)(2,1)S(1)} %reshape.34), channel_id=1, replica_groups=mesh['dp'=8,'mp'=4] {'mp'}, dimensions={0}, use_global_device_ids=true | all-gather | bytes 2560 | tf_op jit(solution)/shard_map/all_gather | solution.py:45
  23.1 2.8 %copy.12 = bf16[4,512,512]{1,2,0:T(8,128)(2,1)S(1)} copy(bf16[4,512,512]{2,1,0:T(8,128)(2,1)} %param.10) | data formatting | bytes 4194304 | tf_op args[4]
  25.9 10.0 %all_gather.15 = bf16[256,1024]{1,0:T(8,128)(2,1)S(1)} all-gather(bf16[256,128]{1,0:T(8,128)(2,1)S(1)} %copy-done.2), channel_id=1, replica_groups=mesh['dp'=8,'mp'=4] {'dp'}, dimensions={1}, use_global_device_ids=true | all-gather | bytes 589824 | tf_op jit(solution)/shard_map/all_gather | solution.py:60
  35.9 6.2 %all-gather.4.cloned.1.call-done = bf16[512,1024]{1,0:T(8,128)(2,1)} async-done(((bf16[512,256]{1,0:T(8,128)(2,1)}), bf16[512,1024]{1,0:T(8,128)(2,1)}) %all-gather.4.cloned.1.call-update) | async-done | bytes 1048592 | tf_op jit(solution)/shard_map/all_gather | solution.py:44
  42.1 1.5 %fusion.2 = f32[512]{0:T(512)S(1)} fusion(bf16[512,1024]{1,0:T(8,128)(2,1)} %all-gather.4.cloned.1.call-done), kind=kLoop, calls=%fused_computation.7 | loop fusion | flops 1572352 | bytes 1050624 | tf_op jit(solution)/shard_map/reduce_sum | solution.py:48
  43.6 25.1 %all-gather.6.cloned.1.call-done = bf16[3,1024,256]{1,2,0:T(8,128)(2,1)} async-done(((bf16[3,128,256]{1,2,0:T(8,128)(2,1)}), bf16[3,1024,256]{1,2,0:T(8,128)(2,1)}) %all-gather.6.cloned.1.call-update) | async-done | bytes 1572880 | tf_op jit(solution)/shard_map/all_gather | solution.py:54
  68.7 2.8 %fusion.6 = bf16[3,512,256]{1,2,0:T(8,128)(2,1)S(1)} fusion(bf16[3,1024,256]{1,2,0:T(8,128)(2,1)} %all-gather.6.cloned.1.call-done, bf16[512,1024]{1,0:T(8,128)(2,1)} %all-gather.4.cloned.1.call-done, f32[1024]{0:T(1024)S(1)} %bitcast.26, f32[512]{0:T(512)S(1)} %add_rsqrt_fusion.1), kind=kOutput, calls=%fused_computation.13 | convolution fusion | flops 807796736 | bytes 3414016 | tf_op jit(solution)/shard_map/td,kdi->kti/dot_general | solution.py:51
  71.5 0.8 fusion.18
  72.3 1.5 %fusion.19 = f32[4,512]{1,0:T(4,128)S(1)} fusion(bf16[4,512,512]{1,2,0:T(8,128)(2,1)S(1)} %copy.12, bf16[512,4,64]{0,2,1:T(8,128)(2,1)S(1)} %bitcast.23, bf16[512,4,64]{0,2,1:T(8,128)(2,1)S(1)} %bitcast.21), kind=kOutput, calls=%fused_computation.29 | convolution fusion | flops 138412544 | bytes 2629632 | tf_op jit(solution)/shard_map/while/body/eval_jaxpr/sub | solution.py:31
  73.8 2.9 %fusion.7 = bf16[4,64,512]{2,1,0:T(8,128)(2,1)S(1)} fusion(bf16[512,4,64]{0,2,1:T(8,128)(2,1)} %bitcast.25, f32[4,512]{1,0:T(4,128)S(1)} %fusion.19, bf16[4,512,512]{1,2,0:T(8,128)(2,1)S(1)} %copy.12, bf16[512,4,64]{0,2,1:T(8,128)(2,1)S(1)} %bitcast.24, bf16[512,4,64]{0,2,1:T(8,128)(2,1)S(1)} %bitcast.22), kind=kOutput, calls=%fused_computation.14 | convolution fusion | flops 273811968 | bytes 3153920 | tf_op jit(solution)/shard_map/while/body/eval_jaxpr/hqk,khd->qhd/dot_general | solution.py:33
  76.6 1.4 %convolution_convert_fusion = bf16[512,1024]{1,0:T(8,128)(2,1)} fusion(bf16[512,256]{0,1:T(8,128)(2,1)S(1)} %bitcast.20, bf16[256,1024]{1,0:T(8,128)(2,1)S(1)} %all_gather.15), kind=kOutput, calls=%fused_computation.11 | convolution fusion | flops 268959744 | bytes 1835008 | tf_op jit(solution)/shard_map/dot_general | solution.py:58
  78.1 0.0 reduce-scatter.2.cloned.1.call-update
  78.1 27.4 %reduce-scatter.2.cloned.1.call-done = bf16[512,256]{1,0:T(8,128)(2,1)} async-done(((bf16[512,1024]{1,0:T(8,128)(2,1)}), bf16[512,256]{1,0:T(8,128)(2,1)}) %reduce-scatter.2.cloned.1.call-update) | async-done | bytes 262160 | tf_op jit(solution)/shard_map/reduce_scatter | solution.py:63
  105.6 1.0 add_convert_fusion
  106.6 0.1 fusion.12
  106.7 9.3 %psum.7 = f32[512]{0:T(512)S(1)} all-reduce(f32[512]{0:T(512)S(1)} %fusion.12), channel_id=1, replica_groups=mesh['dp'=8,'mp'=4] {'mp'}, use_global_device_ids=true, to_apply=%region_5.6 | all-reduce | flops 512 | bytes 4096 | tf_op jit(solution)/shard_map/psum | solution.py:68
  116.0 0.8 fusion.14
  (12 shorter events, 0.0 us)
Async XLA Ops:
  7.2 35.0 %all-gather.4.cloned.1.call-start = ((), (), s32[]{:S(2)}) async-start(), calls=%async_computation.1 | async-start | bytes 1310720 | tf_op jit(solution)/shard_map/all_gather | solution.py:44
  7.9 60.8 %all-gather.6.cloned.1.call-start = ((), (), s32[]{:S(2)}) async-start(), calls=%async_computation.2 | async-start | bytes 1769472 | tf_op jit(solution)/shard_map/all_gather | solution.py:54
  9.7 95.8 %reduce-scatter.2.cloned.1.call-start = ((), (), s32[]{:S(2)}) async-start(), calls=%async_computation.3 | async-start | bytes 1310720 | tf_op jit(solution)/shard_map/reduce_scatter | solution.py:63
  23.1 2.8 %copy-start.2 = (bf16[256,128]{1,0:T(8,128)(2,1)S(1)}, bf16[256,128]{1,0:T(8,128)(2,1)}, u32[]{:S(2)}) copy-start(bf16[256,128]{1,0:T(8,128)(2,1)} %param.9) | copy-start | bytes 196612
  76.6 1.5 %copy-start.3 = (bf16[256]{0:T(256)(128)(2,1)S(1)}, bf16[256]{0:T(256)(128)(2,1)}, u32[]{:S(2)}) copy-start(bf16[256]{0:T(256)(128)(2,1)} %param.11) | copy-start | bytes 1540
  76.6 28.9 %copy-start.1 = (bf16[512,256]{1,0:T(8,128)(2,1)S(1)}, bf16[512,256]{1,0:T(8,128)(2,1)}, u32[]{:S(2)}) copy-start(bf16[512,256]{1,0:T(8,128)(2,1)} %param.6) | copy-start | bytes 786436
  106.6 10.3 %copy-start = (bf16[512,256]{1,0:T(8,128)(2,1)}, bf16[512,256]{1,0:T(8,128)(2,1)S(1)}, u32[]{:S(2)}) copy-start(bf16[512,256]{1,0:T(8,128)(2,1)S(1)} %add_convert_fusion) | copy-start | bytes 786436
Sparse Core Ops, SparseCore 0:
  9.5 32.5 all-gather.3
  44.6 24.0 all-gather.5
  78.2 27.2 reduce-scatter.1
where the time goes:
time: 124 us; the launch traced here: 123 us
  waiting for transfers between devices  59.4 us (48%)
  blocking collectives  31.9 us (26%)
  between operations  13.8 us (11%)
  matrix products  8.6 us (7%)
  local copies, waits for them, and re-layouts  6 us (5%)
  other arithmetic  3.54 us (3%)
    reduce_scatter x1, waiting for transfers between devices, on_device(): lax.psum_scatter(partial_value.astype(jnp.bfloat16), 'mp', scatter_dimens...  27.4 us
    all_gather x1, waiting for transfers between devices, on_device(): lax.all_gather(input_weight, 'dp', axis=1, tiled=True)  25.1 us
    all_gather x1, blocking collectives, on_device(): lax.all_gather(pre_gain, 'mp', axis=0, tiled=True)  12.6 us
    all_gather x1, blocking collectives, on_device(): lax.all_gather(output_weight, 'dp', axis=1, tiled=True)  9.99 us
    psum x1, blocking collectives, on_device(): squares = lax.psum(jnp.sum(restored * restored, axis=1), 'mp')  9.28 us
    all_gather x1, waiting for transfers between devices, on_device(): lax.all_gather(tokens, 'mp', axis=1, tiled=True)  6.23 us
    unnamed x11, local copies, waits for them, and re-layouts  5.24 us
    dot_general x1, matrix products, one_sequence(): jnp.einsum('hqk,khd->qhd', probabilities, sequence_block[2], preferred_el...  2.86 us
  transfers between devices with their start and end apart: 3, of which 3 were waited for; matrix products, arithmetic and copies ran while one was open for 5% of the time, Pallas kernels for 0%

commit v1 on v0

--- a/solution.py
+++ b/solution.py
@@ -51,7 +51,7 @@
     projected = jnp.einsum(
         "td,kdi->kti",
         normed_in,
-        lax.all_gather(input_weight, "dp", axis=1, tiled=True),
+        jnp.concatenate(lax.all_gather(input_weight, "dp"), axis=1),
         preferred_element_type=jnp.float32,
     )
     context = attend_all(projected.astype(jnp.bfloat16), position_bias)

time: 124 us -> 127 us (1.024)
  local copies, waits for them, and re-layouts: 6 us -> 9.66 us
    reshape x0 -> x1, local copies, waits for them, and re-layouts: none -> 2.06 us  [on_device(): jnp.concatenate(lax.all_gather(input_weight, 'dp'), axis=1)]
    all_gather x0 -> x1, local copies, waits for them, and re-layouts: none -> 1.99 us  [on_device(): lax.all_gather(input_weight, 'dp')]
    unnamed x11 -> x12, local copies, waits for them, and re-layouts: 5.24 us -> 4.86 us
where the time goes in v1:
time: 127 us
  waiting for transfers between devices  59.2 us (47%)
  blocking collectives  31.9 us (25%)
  between operations  13.8 us (11%)
  local copies, waits for them, and re-layouts  9.66 us (8%)
  matrix products  8.74 us (7%)
  other arithmetic  3.54 us (3%)
    reduce_scatter x1, waiting for transfers between devices, on_device(): lax.psum_scatter(partial_value.astype(jnp.bfloat16), 'mp', scatter_dimens...  27.4 us
    all_gather x1, waiting for transfers between devices, on_device(): lax.all_gather(input_weight, 'dp')  24.3 us
    all_gather x1, blocking collectives, on_device(): lax.all_gather(pre_gain, 'mp', axis=0, tiled=True)  12.6 us
    all_gather x1, blocking collectives, on_device(): lax.all_gather(output_weight, 'dp', axis=1, tiled=True)  9.97 us
    psum x1, blocking collectives, on_device(): squares = lax.psum(jnp.sum(restored * restored, axis=1), 'mp')  9.27 us
    all_gather x1, waiting for transfers between devices, on_device(): lax.all_gather(tokens, 'mp', axis=1, tiled=True)  6.07 us
    unnamed x12, local copies, waits for them, and re-layouts  4.86 us
    dot_general x1, matrix products, on_device(): jnp.einsum('td,kdi->kti', normed_in, jnp.concatenate(lax.all_gather(input...  2.96 us
  transfers between devices with their start and end apart: 3, of which 3 were waited for; matrix products, arithmetic and copies ran while one was open for 5% of the time, Pallas kernels for 0%

profile of v1, /device:TPU:0, one launch (start us, length us, event | category | flops | bytes accessed | tf_op | source)
XLA Modules:
  0.0 126.9 jit_solution(13989687125198992293)
XLA Ops:
  7.2 0.0 all-gather.5.cloned.1.call-start
  7.2 0.7 all-gather.5.cloned.1.call-update
  7.9 0.0 all-gather.7.cloned.1.call-start
  7.9 0.7 all-gather.7.cloned.1.call-update
  8.6 0.0 reduce-scatter.2.cloned.1.call-start
  8.7 0.7 reshape.43
  9.4 12.6 %all-gather.1 = bf16[4,1,256]{2,1,0:T(2,128)(2,1)S(1)} all-gather(bf16[1,1,256]{2,1,0:T(2,128)(2,1)S(1)} %reshape.43), channel_id=1, replica_groups=mesh['dp'=8,'mp'=4] {'mp'}, dimensions={0}, use_global_device_ids=true | all-gather | bytes 2560 | tf_op jit(solution)/shard_map/all_gather | solution.py:45
  22.0 4.2 %copy.12 = bf16[4,512,512]{1,2,0:T(8,128)(2,1)} copy(bf16[4,512,512]{2,1,0:T(8,128)(2,1)} %param.10) | data formatting | bytes 4194304 | tf_op args[4]
  26.2 10.0 %all_gather.19 = bf16[256,1024]{1,0:T(8,128)(2,1)S(1)} all-gather(bf16[256,128]{1,0:T(8,128)(2,1)S(1)} %copy-done.3), channel_id=1, replica_groups=mesh['dp'=8,'mp'=4] {'dp'}, dimensions={1}, use_global_device_ids=true | all-gather | bytes 589824 | tf_op jit(solution)/shard_map/all_gather | solution.py:60
  36.2 6.1 %all-gather.5.cloned.1.call-done = bf16[512,1024]{1,0:T(8,128)(2,1)} async-done(((bf16[512,256]{1,0:T(8,128)(2,1)}), bf16[512,1024]{1,0:T(8,128)(2,1)}) %all-gather.5.cloned.1.call-update) | async-done | bytes 1048592 | tf_op jit(solution)/shard_map/all_gather | solution.py:44
  42.2 1.5 %fusion.2 = f32[512]{0:T(512)S(1)} fusion(bf16[512,1024]{1,0:T(8,128)(2,1)} %all-gather.5.cloned.1.call-done), kind=kLoop, calls=%fused_computation.7 | loop fusion | flops 1572352 | bytes 1050624 | tf_op jit(solution)/shard_map/reduce_sum | solution.py:48
  43.7 24.3 %all-gather.7.cloned.1.call-done = bf16[24,128,256]{2,1,0:T(8,128)(2,1)} async-done(((bf16[3,128,256]{2,1,0:T(8,128)(2,1)}), bf16[24,128,256]{2,1,0:T(8,128)(2,1)}) %all-gather.7.cloned.1.call-update) | async-done | bytes 1572880 | tf_op jit(solution)/shard_map/all_gather | solution.py:54
  68.0 2.0 %copy.11 = bf16[8,3,128,256]{2,0,3,1:T(8,128)(2,1)S(1)} copy(bf16[8,3,128,256]{3,2,1,0:T(8,128)(2,1)} %bitcast.27) | data formatting | bytes 3145728 | tf_op jit(solution)/shard_map/all_gather | solution.py:54
  70.0 2.1 %reshape.41 = bf16[3,1024,256]{1,2,0:T(8,128)(2,1)} reshape(bf16[3,8,128,256]{2,1,3,0:T(8,128)(2,1)S(1)} %bitcast.26) | data formatting | bytes 3145728 | tf_op jit(solution)/shard_map/reshape | solution.py:54
  72.1 3.0 %fusion.6 = bf16[3,512,256]{1,2,0:T(8,128)(2,1)S(1)} fusion(bf16[3,1024,256]{1,2,0:T(8,128)(2,1)} %reshape.41, bf16[512,1024]{1,0:T(8,128)(2,1)} %all-gather.5.cloned.1.call-done, f32[1024]{0:T(1024)S(1)} %bitcast.34, f32[512]{0:T(512)S(1)} %add_rsqrt_fusion.1), kind=kOutput, calls=%fused_computation.13 | convolution fusion | flops 807796736 | bytes 3414016 | tf_op jit(solution)/shard_map/td,kdi->kti/dot_general | solution.py:51
  75.0 0.8 fusion.18
  75.8 1.5 %fusion.19 = f32[4,512]{1,0:T(4,128)S(1)} fusion(bf16[4,512,512]{1,2,0:T(8,128)(2,1)S(1)} %copy-done.1, bf16[512,4,64]{0,2,1:T(8,128)(2,1)S(1)} %bitcast.31, bf16[512,4,64]{0,2,1:T(8,128)(2,1)S(1)} %bitcast.29), kind=kOutput, calls=%fused_computation.29 | convolution fusion | flops 138412544 | bytes 2629632 | tf_op jit(solution)/shard_map/while/body/eval_jaxpr/sub | solution.py:31
  77.3 2.9 %fusion.7 = bf16[4,64,512]{2,1,0:T(8,128)(2,1)S(1)} fusion(bf16[512,4,64]{0,2,1:T(8,128)(2,1)} %bitcast.33, f32[4,512]{1,0:T(4,128)S(1)} %fusion.19, bf16[4,512,512]{1,2,0:T(8,128)(2,1)S(1)} %copy-done.1, bf16[512,4,64]{0,2,1:T(8,128)(2,1)S(1)} %bitcast.32, bf16[512,4,64]{0,2,1:T(8,128)(2,1)S(1)} %bitcast.30), kind=kOutput, calls=%fused_computation.14 | convolution fusion | flops 273811968 | bytes 3153920 | tf_op jit(solution)/shard_map/while/body/eval_jaxpr/hqk,khd->qhd/dot_general | solution.py:33
  80.2 1.4 %convolution_convert_fusion = bf16[512,1024]{1,0:T(8,128)(2,1)} fusion(bf16[512,256]{0,1:T(8,128)(2,1)S(1)} %bitcast.28, bf16[256,1024]{1,0:T(8,128)(2,1)S(1)} %all_gather.19), kind=kOutput, calls=%fused_computation.11 | convolution fusion | flops 268959744 | bytes 1835008 | tf_op jit(solution)/shard_map/dot_general | solution.py:58
  81.7 27.4 %reduce-scatter.2.cloned.1.call-done = bf16[512,256]{1,0:T(8,128)(2,1)} async-done(((bf16[512,1024]{1,0:T(8,128)(2,1)}), bf16[512,256]{1,0:T(8,128)(2,1)}) %reduce-scatter.2.cloned.1.call-update) | async-done | bytes 262160 | tf_op jit(solution)/shard_map/reduce_scatter | solution.py:63
  109.1 1.0 add_convert_fusion
  110.1 0.1 fusion.12
  110.3 9.3 %psum.7 = f32[512]{0:T(512)S(1)} all-reduce(f32[512]{0:T(512)S(1)} %fusion.12), channel_id=1, replica_groups=mesh['dp'=8,'mp'=4] {'mp'}, use_global_device_ids=true, to_apply=%region_5.6 | all-reduce | flops 512 | bytes 4096 | tf_op jit(solution)/shard_map/psum | solution.py:68
  119.5 0.8 fusion.14
  (15 shorter events, 0.1 us)
Async XLA Ops:
  7.2 35.1 %all-gather.5.cloned.1.call-start = ((), (), s32[]{:S(2)}) async-start(), calls=%async_computation.1 | async-start | bytes 1310720 | tf_op jit(solution)/shard_map/all_gather | solution.py:44
  7.9 60.1 %all-gather.7.cloned.1.call-start = ((), (), s32[]{:S(2)}) async-start(), calls=%async_computation.3 | async-start | bytes 1769472 | tf_op jit(solution)/shard_map/all_gather | solution.py:54
  8.6 100.4 %reduce-scatter.2.cloned.1.call-start = ((), (), s32[]{:S(2)}) async-start(), calls=%async_computation.2 | async-start | bytes 1310720 | tf_op jit(solution)/shard_map/reduce_scatter | solution.py:63
  22.0 4.2 %copy-start.3 = (bf16[256,128]{1,0:T(8,128)(2,1)S(1)}, bf16[256,128]{1,0:T(8,128)(2,1)}, u32[]{:S(2)}) copy-start(bf16[256,128]{1,0:T(8,128)(2,1)} %param.9) | copy-start | bytes 196612
  72.1 3.7 %copy-start.1 = (bf16[4,512,512]{1,2,0:T(8,128)(2,1)S(1)}, bf16[4,512,512]{1,2,0:T(8,128)(2,1)}, u32[]{:S(2)}) copy-start(bf16[4,512,512]{1,2,0:T(8,128)(2,1)} %copy.12) | copy-start | bytes 6291460
  80.1 1.5 %copy-start.4 = (bf16[256]{0:T(256)(128)(2,1)S(1)}, bf16[256]{0:T(256)(128)(2,1)}, u32[]{:S(2)}) copy-start(bf16[256]{0:T(256)(128)(2,1)} %param.11) | copy-start | bytes 1540
  80.1 28.9 %copy-start.2 = (bf16[512,256]{1,0:T(8,128)(2,1)S(1)}, bf16[512,256]{1,0:T(8,128)(2,1)}, u32[]{:S(2)}) copy-start(bf16[512,256]{1,0:T(8,128)(2,1)} %param.6) | copy-start | bytes 786436
  110.1 10.3 %copy-start = (bf16[512,256]{1,0:T(8,128)(2,1)}, bf16[512,256]{1,0:T(8,128)(2,1)S(1)}, u32[]{:S(2)}) copy-start(bf16[512,256]{1,0:T(8,128)(2,1)S(1)} %add_convert_fusion) | copy-start | bytes 786436
Sparse Core Ops, SparseCore 0:
  9.5 32.6 all-gather.4
  44.1 23.8 all-gather.6
  81.8 27.2 reduce-scatter.1
